TPU v7x, 64 devices: a 2x2x8 block of a 4x4x8 slice. The times are simulated.
64 devices in a mesh: dp: 4 (over x, y), cp: 16 (over z, core).
Axes of the slice: x: 2, y: 2, z: 8, core: 2. Of those that a mesh axis runs over, the one named last changes fastest.
The devices are a block of a 4x4x8 slice.
Arguments:
- query: bfloat16 [12, 768, 22, 128], P('dp', 'cp'), parts along dimension 0
- key: bfloat16 [12, 768, 128], P('dp', 'cp'), parts along dimension 0
- value: bfloat16 [12, 768, 128], P('dp', 'cp'), parts along dimension 0
- positions: int32 [3072], P(('dp', 'cp')), parts along dimension 0
- grad_out: bfloat16 [12, 768, 22, 128], P('dp', 'cp'), parts along dimension 0
Outputs:
- output 1: bfloat16 [12, 768, 22, 128], P('dp', 'cp'), parts along dimension 0
- output 2: bfloat16 [12, 768, 22, 128], P('dp', 'cp'), parts along dimension 0
- output 3: bfloat16 [12, 768, 128], P('dp', 'cp'), parts along dimension 0
- output 4: bfloat16 [12, 768, 128], P('dp', 'cp'), parts along dimension 0
There are 4 independent parts. A program takes and returns all parts, laid end to end along the dimension named above; each array names one.
All inputs are finite; a program needn't handle non-finite values.
Results may differ from a plain program's by a relative error of at most 0.00821643.
Values are sent between devices in bfloat16 or wider.
A program may use at most 768 MiB of HBM per device.

v0:
```python
import jax
import jax.numpy as jnp
from jax import lax
from jax.sharding import PartitionSpec as P

ROPE_BASE = 10000


def rope_tables(positions, head):
    half_dim = head // 2
    inv_freq = jnp.power(jnp.float32(ROPE_BASE), -2.0 * jnp.arange(half_dim, dtype=jnp.float32) / head)
    angles = positions.astype(jnp.float32)[..., None] * inv_freq
    angles = jnp.concatenate([angles, angles], axis=-1)
    return jnp.cos(angles), jnp.sin(angles)


def rotate(values, cos_tab, sin_tab):
    half_dim = values.shape[-1] // 2
    turned = jnp.concatenate([-values[..., half_dim:], values[..., :half_dim]], axis=-1)
    return values * cos_tab + turned * sin_tab


def solution(mesh):
    cp_size = mesh.shape['cp']
    shift_pairs = [(source, (source + 1) % cp_size) for source in range(cp_size)]
    query_spec = P('dp', 'cp', None, None)
    kv_spec = P('dp', 'cp', None)
    pos_spec = P(('dp', 'cp'))

    def per_device(query, key, value, positions, grad_out):
        batch, blk_len, heads, head = query.shape
        scale = head ** -0.5
        my_idx = lax.axis_index('cp')
        cos_tab, sin_tab = rope_tables(positions, head)
        cos_q = cos_tab[None, :, None, :]
        sin_q = sin_tab[None, :, None, :]
        query_rot = rotate(query, cos_q, sin_q).astype(jnp.bfloat16)
        key_rot = rotate(key, cos_tab[None], sin_tab[None]).astype(jnp.bfloat16)
        local_idx = jnp.arange(blk_len)
        diag_mask = (local_idx[None, :] <= local_idx[:, None])[None, :, None, :]

        def block_scores(key_blk, causal_mask):
            scores = jnp.einsum('crie,cle->cril', query_rot, key_blk, preferred_element_type=jnp.float32) * scale
            if causal_mask is None:
                return scores
            return jnp.where(causal_mask, scores, -jnp.inf)

        def forward_block(key_blk, value_blk, state, causal_mask):
            run_max, run_sum, out_acc = state
            scores = block_scores(key_blk, causal_mask)
            new_max = jnp.maximum(run_max, jnp.max(scores, axis=-1))
            factor = jnp.exp(run_max - new_max)
            weights = jnp.exp(scores - new_max[..., None])
            run_sum = run_sum * factor + jnp.sum(weights, axis=-1)
            out_acc = out_acc * factor[..., None] + jnp.einsum('cril,cle->crie', weights.astype(jnp.bfloat16), value_blk, preferred_element_type=jnp.float32)
            return new_max, run_sum, out_acc

        init_state = (jnp.full((batch, blk_len, heads), -jnp.inf, jnp.float32), jnp.zeros((batch, blk_len, heads), jnp.float32), jnp.zeros((batch, blk_len, heads, head), jnp.float32))
        state = forward_block(key_rot, value, init_state, diag_mask)

        def forward_step(step, carry):
            key_blk, value_blk, state_in = carry
            key_blk, value_blk = lax.ppermute((key_blk, value_blk), 'cp', shift_pairs)
            state_out = lax.cond(step <= my_idx, lambda prev: forward_block(key_blk, value_blk, prev, None), lambda prev: prev, state_in)
            return key_blk, value_blk, state_out

        fwd_carry = lax.fori_loop(1, cp_size, forward_step, (key_rot, value, state))
        run_max, run_sum, out_acc = fwd_carry[2]
        attn_out = (out_acc / run_sum[..., None]).astype(jnp.bfloat16)
        log_sum = run_max + jnp.log(run_sum)
        delta = jnp.einsum('bqhd,bqhd->bqh', grad_out, attn_out, preferred_element_type=jnp.float32)

        def backward_block(key_blk, value_blk, grads, causal_mask):
            dquery_acc, dkey_blk, dvalue_blk = grads
            scores = block_scores(key_blk, causal_mask)
            probs_f = jnp.exp(scores - log_sum[..., None])
            dprobs = jnp.einsum('crie,cle->cril', grad_out, value_blk, preferred_element_type=jnp.float32)
            dscore = (probs_f * (dprobs - delta[..., None])).astype(jnp.bfloat16)
            dquery_acc = dquery_acc + jnp.einsum('cril,cle->crie', dscore, key_blk, preferred_element_type=jnp.float32) * scale
            dkey_blk = dkey_blk + jnp.einsum('cril,crie->cle', dscore, query_rot, preferred_element_type=jnp.float32) * scale
            dvalue_blk = dvalue_blk + jnp.einsum('cril,crie->cle', probs_f.astype(jnp.bfloat16), grad_out, preferred_element_type=jnp.float32)
            return dquery_acc, dkey_blk, dvalue_blk

        zero_kv = jnp.zeros((batch, blk_len, head), jnp.float32)
        grads = backward_block(key_rot, value, (jnp.zeros((batch, blk_len, heads, head), jnp.float32), zero_kv, zero_kv), diag_mask)

        def backward_step(step, carry):
            key_blk, value_blk, dquery_acc, dkey_blk, dvalue_blk = carry
            key_blk, value_blk, dkey_blk, dvalue_blk = lax.ppermute((key_blk, value_blk, dkey_blk, dvalue_blk), 'cp', shift_pairs)
            grads_new = lax.cond(step <= my_idx, lambda prev: backward_block(key_blk, value_blk, prev, None), lambda prev: prev, (dquery_acc, dkey_blk, dvalue_blk))
            return (key_blk, value_blk) + tuple(grads_new)

        bwd_carry = lax.fori_loop(1, cp_size, backward_step, (key_rot, value) + tuple(grads))
        dkey_home, dvalue_home = lax.ppermute((bwd_carry[3], bwd_carry[4]), 'cp', shift_pairs)
        grad_query = rotate(bwd_carry[2], cos_q, -sin_q).astype(jnp.bfloat16)
        grad_key = rotate(dkey_home, cos_tab[None], -sin_tab[None]).astype(jnp.bfloat16)
        return attn_out, grad_query, grad_key, dvalue_home.astype(jnp.bfloat16)

    return jax.shard_map(per_device, mesh=mesh, in_specs=(query_spec, kv_spec, kv_spec, pos_spec, query_spec), out_specs=(query_spec, query_spec, kv_spec, kv_spec), check_vma=False)
```

profile of v0, /device:TPU:119, one launch (start us, length us, event | category | flops | bytes accessed | tf_op | source)
XLA Modules:
  0.0 276.8 jit_solution(7065853805404769852)
XLA Ops:
  12.5 97.0 %while.42 = (s32[]{:T(128)}, bf16[3,48,128]{2,1,0:T(8,128)(2,1)S(1)}, bf16[3,48,128]{2,1,0:T(8,128)(2,1)S(1)}, f32[3,48,22]{1,2,0:T(8,128)S(1)}, f32[3,48,22]{1,...) while((s32[]{:T(128)}, ...), condition=%wide.region_7.8_spmd, body=%wide.region_2.7_spmd.sunk | while | flops 79890624 | bytes 6598947 | solution.py:67
  20.2 3.6 %collective-permute-start = (bf16[3,48,128]{2,1,0:T(8,128)(2,1)S(1)}, bf16[3,48,128]{2,1,0:T(8,128)(2,1)S(1)}, u32[]{:S(2)}, u32[]{:S(2)}) collective-permute-start(bf16[3,48,128]{2,1,0:T(8,128)(2,1)S(1)} %get-tuple-element.621), channel_id=1, source_target_pairs={{0,1},{1,2},{2,3},{3,4},{4,5},{5,6},{6,7},{7,8},{8,9},{9,10},{10,1... | collective-permute-start | bytes 110600 | tf_op jit(solution)/shard_map/while/body/eval_jaxpr/ppermute | solution.py:63
  27.9 3.6 %collective-permute-start = (bf16[3,48,128]{2,1,0:T(8,128)(2,1)S(1)}, bf16[3,48,128]{2,1,0:T(8,128)(2,1)S(1)}, u32[]{:S(2)}, u32[]{:S(2)}) collective-permute-start(bf16[3,48,128]{2,1,0:T(8,128)(2,1)S(1)} %get-tuple-element.621), channel_id=1, source_target_pairs={{0,1},{1,2},{2,3},{3,4},{4,5},{5,6},{6,7},{7,8},{8,9},{9,10},{10,1... | collective-permute-start | bytes 110600 | tf_op jit(solution)/shard_map/while/body/eval_jaxpr/ppermute | solution.py:63
  35.6 3.6 %collective-permute-start = (bf16[3,48,128]{2,1,0:T(8,128)(2,1)S(1)}, bf16[3,48,128]{2,1,0:T(8,128)(2,1)S(1)}, u32[]{:S(2)}, u32[]{:S(2)}) collective-permute-start(bf16[3,48,128]{2,1,0:T(8,128)(2,1)S(1)} %get-tuple-element.621), channel_id=1, source_target_pairs={{0,1},{1,2},{2,3},{3,4},{4,5},{5,6},{6,7},{7,8},{8,9},{9,10},{10,1... | collective-permute-start | bytes 110600 | tf_op jit(solution)/shard_map/while/body/eval_jaxpr/ppermute | solution.py:63
  43.3 3.6 %collective-permute-start = (bf16[3,48,128]{2,1,0:T(8,128)(2,1)S(1)}, bf16[3,48,128]{2,1,0:T(8,128)(2,1)S(1)}, u32[]{:S(2)}, u32[]{:S(2)}) collective-permute-start(bf16[3,48,128]{2,1,0:T(8,128)(2,1)S(1)} %get-tuple-element.621), channel_id=1, source_target_pairs={{0,1},{1,2},{2,3},{3,4},{4,5},{5,6},{6,7},{7,8},{8,9},{9,10},{10,1... | collective-permute-start | bytes 110600 | tf_op jit(solution)/shard_map/while/body/eval_jaxpr/ppermute | solution.py:63
  51.0 3.6 %collective-permute-start = (bf16[3,48,128]{2,1,0:T(8,128)(2,1)S(1)}, bf16[3,48,128]{2,1,0:T(8,128)(2,1)S(1)}, u32[]{:S(2)}, u32[]{:S(2)}) collective-permute-start(bf16[3,48,128]{2,1,0:T(8,128)(2,1)S(1)} %get-tuple-element.621), channel_id=1, source_target_pairs={{0,1},{1,2},{2,3},{3,4},{4,5},{5,6},{6,7},{7,8},{8,9},{9,10},{10,1... | collective-permute-start | bytes 110600 | tf_op jit(solution)/shard_map/while/body/eval_jaxpr/ppermute | solution.py:63
  58.7 3.6 %collective-permute-start = (bf16[3,48,128]{2,1,0:T(8,128)(2,1)S(1)}, bf16[3,48,128]{2,1,0:T(8,128)(2,1)S(1)}, u32[]{:S(2)}, u32[]{:S(2)}) collective-permute-start(bf16[3,48,128]{2,1,0:T(8,128)(2,1)S(1)} %get-tuple-element.621), channel_id=1, source_target_pairs={{0,1},{1,2},{2,3},{3,4},{4,5},{5,6},{6,7},{7,8},{8,9},{9,10},{10,1... | collective-permute-start | bytes 110600 | tf_op jit(solution)/shard_map/while/body/eval_jaxpr/ppermute | solution.py:63
  66.4 3.6 %collective-permute-start = (bf16[3,48,128]{2,1,0:T(8,128)(2,1)S(1)}, bf16[3,48,128]{2,1,0:T(8,128)(2,1)S(1)}, u32[]{:S(2)}, u32[]{:S(2)}) collective-permute-start(bf16[3,48,128]{2,1,0:T(8,128)(2,1)S(1)} %get-tuple-element.621), channel_id=1, source_target_pairs={{0,1},{1,2},{2,3},{3,4},{4,5},{5,6},{6,7},{7,8},{8,9},{9,10},{10,1... | collective-permute-start | bytes 110600 | tf_op jit(solution)/shard_map/while/body/eval_jaxpr/ppermute | solution.py:63
  71.5 6.3 %collective-permute-start = (bf16[3,48,128]{2,1,0:T(8,128)(2,1)S(1)}, bf16[3,48,128]{2,1,0:T(8,128)(2,1)S(1)}, u32[]{:S(2)}, u32[]{:S(2)}) collective-permute-start(bf16[3,48,128]{2,1,0:T(8,128)(2,1)S(1)} %get-tuple-element.621), channel_id=1, source_target_pairs={{0,1},{1,2},{2,3},{3,4},{4,5},{5,6},{6,7},{7,8},{8,9},{9,10},{10,1... | collective-permute-start | bytes 110600 | tf_op jit(solution)/shard_map/while/body/eval_jaxpr/ppermute | solution.py:63
  79.2 3.6 %collective-permute-start = (bf16[3,48,128]{2,1,0:T(8,128)(2,1)S(1)}, bf16[3,48,128]{2,1,0:T(8,128)(2,1)S(1)}, u32[]{:S(2)}, u32[]{:S(2)}) collective-permute-start(bf16[3,48,128]{2,1,0:T(8,128)(2,1)S(1)} %get-tuple-element.621), channel_id=1, source_target_pairs={{0,1},{1,2},{2,3},{3,4},{4,5},{5,6},{6,7},{7,8},{8,9},{9,10},{10,1... | collective-permute-start | bytes 110600 | tf_op jit(solution)/shard_map/while/body/eval_jaxpr/ppermute | solution.py:63
  84.2 3.6 %collective-permute-start = (bf16[3,48,128]{2,1,0:T(8,128)(2,1)S(1)}, bf16[3,48,128]{2,1,0:T(8,128)(2,1)S(1)}, u32[]{:S(2)}, u32[]{:S(2)}) collective-permute-start(bf16[3,48,128]{2,1,0:T(8,128)(2,1)S(1)} %get-tuple-element.621), channel_id=1, source_target_pairs={{0,1},{1,2},{2,3},{3,4},{4,5},{5,6},{6,7},{7,8},{8,9},{9,10},{10,1... | collective-permute-start | bytes 110600 | tf_op jit(solution)/shard_map/while/body/eval_jaxpr/ppermute | solution.py:63
  89.3 3.6 %collective-permute-start = (bf16[3,48,128]{2,1,0:T(8,128)(2,1)S(1)}, bf16[3,48,128]{2,1,0:T(8,128)(2,1)S(1)}, u32[]{:S(2)}, u32[]{:S(2)}) collective-permute-start(bf16[3,48,128]{2,1,0:T(8,128)(2,1)S(1)} %get-tuple-element.621), channel_id=1, source_target_pairs={{0,1},{1,2},{2,3},{3,4},{4,5},{5,6},{6,7},{7,8},{8,9},{9,10},{10,1... | collective-permute-start | bytes 110600 | tf_op jit(solution)/shard_map/while/body/eval_jaxpr/ppermute | solution.py:63
  94.4 3.6 %collective-permute-start = (bf16[3,48,128]{2,1,0:T(8,128)(2,1)S(1)}, bf16[3,48,128]{2,1,0:T(8,128)(2,1)S(1)}, u32[]{:S(2)}, u32[]{:S(2)}) collective-permute-start(bf16[3,48,128]{2,1,0:T(8,128)(2,1)S(1)} %get-tuple-element.621), channel_id=1, source_target_pairs={{0,1},{1,2},{2,3},{3,4},{4,5},{5,6},{6,7},{7,8},{8,9},{9,10},{10,1... | collective-permute-start | bytes 110600 | tf_op jit(solution)/shard_map/while/body/eval_jaxpr/ppermute | solution.py:63
  99.4 3.6 %collective-permute-start = (bf16[3,48,128]{2,1,0:T(8,128)(2,1)S(1)}, bf16[3,48,128]{2,1,0:T(8,128)(2,1)S(1)}, u32[]{:S(2)}, u32[]{:S(2)}) collective-permute-start(bf16[3,48,128]{2,1,0:T(8,128)(2,1)S(1)} %get-tuple-element.621), channel_id=1, source_target_pairs={{0,1},{1,2},{2,3},{3,4},{4,5},{5,6},{6,7},{7,8},{8,9},{9,10},{10,1... | collective-permute-start | bytes 110600 | tf_op jit(solution)/shard_map/while/body/eval_jaxpr/ppermute | solution.py:63
  104.5 3.6 %collective-permute-start = (bf16[3,48,128]{2,1,0:T(8,128)(2,1)S(1)}, bf16[3,48,128]{2,1,0:T(8,128)(2,1)S(1)}, u32[]{:S(2)}, u32[]{:S(2)}) collective-permute-start(bf16[3,48,128]{2,1,0:T(8,128)(2,1)S(1)} %get-tuple-element.621), channel_id=1, source_target_pairs={{0,1},{1,2},{2,3},{3,4},{4,5},{5,6},{6,7},{7,8},{8,9},{9,10},{10,1... | collective-permute-start | bytes 110600 | tf_op jit(solution)/shard_map/while/body/eval_jaxpr/ppermute | solution.py:63
  117.7 150.9 %while.43 = (s32[]{:T(128)}, bf16[3,48,128]{2,1,0:T(8,128)(2,1)}, bf16[3,48,128]{2,1,0:T(8,128)(2,1)}, f32[3,48,22,128]{3,1,2,0:T(8,128)S(1)}, f32[3,48,128]{2,1...) while((s32[]{:T(128)}, bf16[3,48,128]{2,1,0:T(8,128)(2,1)}, ...), condition=%wide.region_11.12_spmd, body=%wide.region_8.11_spmd.sunk | while | flops 196420608 | bytes 10983587 | solution.py:93
  117.7 3.6 %collective-permute-start.4 = (f32[3,48,128]{2,1,0:T(8,128)}, f32[3,48,128]{2,1,0:T(8,128)S(1)}, u32[]{:S(2)}, u32[]{:S(2)}) collective-permute-start(f32[3,48,128]{2,1,0:T(8,128)} %get-tuple-element.654), channel_id=1, source_target_pairs={{0,1},{1,2},{2,3},{3,4},{4,5},{5,6},{6,7},{7,8},{8,9},{9,10},{10,1... | collective-permute-start | bytes 221192 | tf_op jit(solution)/shard_map/while/body/eval_jaxpr/ppermute | solution.py:89
  128.8 3.7 %collective-permute-start.4 = (f32[3,48,128]{2,1,0:T(8,128)}, f32[3,48,128]{2,1,0:T(8,128)S(1)}, u32[]{:S(2)}, u32[]{:S(2)}) collective-permute-start(f32[3,48,128]{2,1,0:T(8,128)} %get-tuple-element.654), channel_id=1, source_target_pairs={{0,1},{1,2},{2,3},{3,4},{4,5},{5,6},{6,7},{7,8},{8,9},{9,10},{10,1... | collective-permute-start | bytes 221192 | tf_op jit(solution)/shard_map/while/body/eval_jaxpr/ppermute | solution.py:89
  140.1 3.7 %collective-permute-start.4 = (f32[3,48,128]{2,1,0:T(8,128)}, f32[3,48,128]{2,1,0:T(8,128)S(1)}, u32[]{:S(2)}, u32[]{:S(2)}) collective-permute-start(f32[3,48,128]{2,1,0:T(8,128)} %get-tuple-element.654), channel_id=1, source_target_pairs={{0,1},{1,2},{2,3},{3,4},{4,5},{5,6},{6,7},{7,8},{8,9},{9,10},{10,1... | collective-permute-start | bytes 221192 | tf_op jit(solution)/shard_map/while/body/eval_jaxpr/ppermute | solution.py:89
  151.4 3.7 %collective-permute-start.4 = (f32[3,48,128]{2,1,0:T(8,128)}, f32[3,48,128]{2,1,0:T(8,128)S(1)}, u32[]{:S(2)}, u32[]{:S(2)}) collective-permute-start(f32[3,48,128]{2,1,0:T(8,128)} %get-tuple-element.654), channel_id=1, source_target_pairs={{0,1},{1,2},{2,3},{3,4},{4,5},{5,6},{6,7},{7,8},{8,9},{9,10},{10,1... | collective-permute-start | bytes 221192 | tf_op jit(solution)/shard_map/while/body/eval_jaxpr/ppermute | solution.py:89
  162.7 3.7 %collective-permute-start.4 = (f32[3,48,128]{2,1,0:T(8,128)}, f32[3,48,128]{2,1,0:T(8,128)S(1)}, u32[]{:S(2)}, u32[]{:S(2)}) collective-permute-start(f32[3,48,128]{2,1,0:T(8,128)} %get-tuple-element.654), channel_id=1, source_target_pairs={{0,1},{1,2},{2,3},{3,4},{4,5},{5,6},{6,7},{7,8},{8,9},{9,10},{10,1... | collective-permute-start | bytes 221192 | tf_op jit(solution)/shard_map/while/body/eval_jaxpr/ppermute | solution.py:89
  173.9 3.7 %collective-permute-start.4 = (f32[3,48,128]{2,1,0:T(8,128)}, f32[3,48,128]{2,1,0:T(8,128)S(1)}, u32[]{:S(2)}, u32[]{:S(2)}) collective-permute-start(f32[3,48,128]{2,1,0:T(8,128)} %get-tuple-element.654), channel_id=1, source_target_pairs={{0,1},{1,2},{2,3},{3,4},{4,5},{5,6},{6,7},{7,8},{8,9},{9,10},{10,1... | collective-permute-start | bytes 221192 | tf_op jit(solution)/shard_map/while/body/eval_jaxpr/ppermute | solution.py:89
  185.2 3.7 %collective-permute-start.4 = (f32[3,48,128]{2,1,0:T(8,128)}, f32[3,48,128]{2,1,0:T(8,128)S(1)}, u32[]{:S(2)}, u32[]{:S(2)}) collective-permute-start(f32[3,48,128]{2,1,0:T(8,128)} %get-tuple-element.654), channel_id=1, source_target_pairs={{0,1},{1,2},{2,3},{3,4},{4,5},{5,6},{6,7},{7,8},{8,9},{9,10},{10,1... | collective-permute-start | bytes 221192 | tf_op jit(solution)/shard_map/while/body/eval_jaxpr/ppermute | solution.py:89
  196.5 3.7 %collective-permute-start.4 = (f32[3,48,128]{2,1,0:T(8,128)}, f32[3,48,128]{2,1,0:T(8,128)S(1)}, u32[]{:S(2)}, u32[]{:S(2)}) collective-permute-start(f32[3,48,128]{2,1,0:T(8,128)} %get-tuple-element.654), channel_id=1, source_target_pairs={{0,1},{1,2},{2,3},{3,4},{4,5},{5,6},{6,7},{7,8},{8,9},{9,10},{10,1... | collective-permute-start | bytes 221192 | tf_op jit(solution)/shard_map/while/body/eval_jaxpr/ppermute | solution.py:89
  205.2 6.3 %collective-permute-start.4 = (f32[3,48,128]{2,1,0:T(8,128)}, f32[3,48,128]{2,1,0:T(8,128)S(1)}, u32[]{:S(2)}, u32[]{:S(2)}) collective-permute-start(f32[3,48,128]{2,1,0:T(8,128)} %get-tuple-element.654), channel_id=1, source_target_pairs={{0,1},{1,2},{2,3},{3,4},{4,5},{5,6},{6,7},{7,8},{8,9},{9,10},{10,1... | collective-permute-start | bytes 221192 | tf_op jit(solution)/shard_map/while/body/eval_jaxpr/ppermute | solution.py:89
  216.5 3.7 %collective-permute-start.4 = (f32[3,48,128]{2,1,0:T(8,128)}, f32[3,48,128]{2,1,0:T(8,128)S(1)}, u32[]{:S(2)}, u32[]{:S(2)}) collective-permute-start(f32[3,48,128]{2,1,0:T(8,128)} %get-tuple-element.654), channel_id=1, source_target_pairs={{0,1},{1,2},{2,3},{3,4},{4,5},{5,6},{6,7},{7,8},{8,9},{9,10},{10,1... | collective-permute-start | bytes 221192 | tf_op jit(solution)/shard_map/while/body/eval_jaxpr/ppermute | solution.py:89
  225.2 3.7 %collective-permute-start.4 = (f32[3,48,128]{2,1,0:T(8,128)}, f32[3,48,128]{2,1,0:T(8,128)S(1)}, u32[]{:S(2)}, u32[]{:S(2)}) collective-permute-start(f32[3,48,128]{2,1,0:T(8,128)} %get-tuple-element.654), channel_id=1, source_target_pairs={{0,1},{1,2},{2,3},{3,4},{4,5},{5,6},{6,7},{7,8},{8,9},{9,10},{10,1... | collective-permute-start | bytes 221192 | tf_op jit(solution)/shard_map/while/body/eval_jaxpr/ppermute | solution.py:89
  233.8 3.7 %collective-permute-start.4 = (f32[3,48,128]{2,1,0:T(8,128)}, f32[3,48,128]{2,1,0:T(8,128)S(1)}, u32[]{:S(2)}, u32[]{:S(2)}) collective-permute-start(f32[3,48,128]{2,1,0:T(8,128)} %get-tuple-element.654), channel_id=1, source_target_pairs={{0,1},{1,2},{2,3},{3,4},{4,5},{5,6},{6,7},{7,8},{8,9},{9,10},{10,1... | collective-permute-start | bytes 221192 | tf_op jit(solution)/shard_map/while/body/eval_jaxpr/ppermute | solution.py:89
  242.5 3.7 %collective-permute-start.4 = (f32[3,48,128]{2,1,0:T(8,128)}, f32[3,48,128]{2,1,0:T(8,128)S(1)}, u32[]{:S(2)}, u32[]{:S(2)}) collective-permute-start(f32[3,48,128]{2,1,0:T(8,128)} %get-tuple-element.654), channel_id=1, source_target_pairs={{0,1},{1,2},{2,3},{3,4},{4,5},{5,6},{6,7},{7,8},{8,9},{9,10},{10,1... | collective-permute-start | bytes 221192 | tf_op jit(solution)/shard_map/while/body/eval_jaxpr/ppermute | solution.py:89
  251.2 3.7 %collective-permute-start.4 = (f32[3,48,128]{2,1,0:T(8,128)}, f32[3,48,128]{2,1,0:T(8,128)S(1)}, u32[]{:S(2)}, u32[]{:S(2)}) collective-permute-start(f32[3,48,128]{2,1,0:T(8,128)} %get-tuple-element.654), channel_id=1, source_target_pairs={{0,1},{1,2},{2,3},{3,4},{4,5},{5,6},{6,7},{7,8},{8,9},{9,10},{10,1... | collective-permute-start | bytes 221192 | tf_op jit(solution)/shard_map/while/body/eval_jaxpr/ppermute | solution.py:89
  259.9 3.7 %collective-permute-start.4 = (f32[3,48,128]{2,1,0:T(8,128)}, f32[3,48,128]{2,1,0:T(8,128)S(1)}, u32[]{:S(2)}, u32[]{:S(2)}) collective-permute-start(f32[3,48,128]{2,1,0:T(8,128)} %get-tuple-element.654), channel_id=1, source_target_pairs={{0,1},{1,2},{2,3},{3,4},{4,5},{5,6},{6,7},{7,8},{8,9},{9,10},{10,1... | collective-permute-start | bytes 221192 | tf_op jit(solution)/shard_map/while/body/eval_jaxpr/ppermute | solution.py:89
  268.6 3.7 %collective-permute-start.6 = (f32[3,48,128]{2,1,0:T(8,128)}, f32[3,48,128]{2,1,0:T(8,128)S(1)}, u32[]{:S(2)}, u32[]{:S(2)}) collective-permute-start(f32[3,48,128]{2,1,0:T(8,128)} %get-tuple-element.410), channel_id=1, source_target_pairs={{0,1},{1,2},{2,3},{3,4},{4,5},{5,6},{6,7},{7,8},{8,9},{9,10},{10,1... | collective-permute-start | bytes 221192 | tf_op jit(solution)/shard_map/ppermute | solution.py:94
  (395 shorter events, 195.9 us)
Async XLA Ops:
  12.5 4.7 %collective-permute-start = (bf16[3,48,128]{2,1,0:T(8,128)(2,1)S(1)}, bf16[3,48,128]{2,1,0:T(8,128)(2,1)S(1)}, u32[]{:S(2)}, u32[]{:S(2)}) collective-permute-start(bf16[3,48,128]{2,1,0:T(8,128)(2,1)S(1)} %get-tuple-element.621), channel_id=1, source_target_pairs={{0,1},{1,2},{2,3},{3,4},{4,5},{5,6},{6,7},{7,8},{8,9},{9,10},{10,1... | collective-permute-start | bytes 110600 | tf_op jit(solution)/shard_map/while/body/eval_jaxpr/ppermute | solution.py:63
  20.2 4.7 %collective-permute-start = (bf16[3,48,128]{2,1,0:T(8,128)(2,1)S(1)}, bf16[3,48,128]{2,1,0:T(8,128)(2,1)S(1)}, u32[]{:S(2)}, u32[]{:S(2)}) collective-permute-start(bf16[3,48,128]{2,1,0:T(8,128)(2,1)S(1)} %get-tuple-element.621), channel_id=1, source_target_pairs={{0,1},{1,2},{2,3},{3,4},{4,5},{5,6},{6,7},{7,8},{8,9},{9,10},{10,1... | collective-permute-start | bytes 110600 | tf_op jit(solution)/shard_map/while/body/eval_jaxpr/ppermute | solution.py:63
  27.9 4.7 %collective-permute-start = (bf16[3,48,128]{2,1,0:T(8,128)(2,1)S(1)}, bf16[3,48,128]{2,1,0:T(8,128)(2,1)S(1)}, u32[]{:S(2)}, u32[]{:S(2)}) collective-permute-start(bf16[3,48,128]{2,1,0:T(8,128)(2,1)S(1)} %get-tuple-element.621), channel_id=1, source_target_pairs={{0,1},{1,2},{2,3},{3,4},{4,5},{5,6},{6,7},{7,8},{8,9},{9,10},{10,1... | collective-permute-start | bytes 110600 | tf_op jit(solution)/shard_map/while/body/eval_jaxpr/ppermute | solution.py:63
  35.6 4.7 %collective-permute-start = (bf16[3,48,128]{2,1,0:T(8,128)(2,1)S(1)}, bf16[3,48,128]{2,1,0:T(8,128)(2,1)S(1)}, u32[]{:S(2)}, u32[]{:S(2)}) collective-permute-start(bf16[3,48,128]{2,1,0:T(8,128)(2,1)S(1)} %get-tuple-element.621), channel_id=1, source_target_pairs={{0,1},{1,2},{2,3},{3,4},{4,5},{5,6},{6,7},{7,8},{8,9},{9,10},{10,1... | collective-permute-start | bytes 110600 | tf_op jit(solution)/shard_map/while/body/eval_jaxpr/ppermute | solution.py:63
  43.3 4.7 %collective-permute-start = (bf16[3,48,128]{2,1,0:T(8,128)(2,1)S(1)}, bf16[3,48,128]{2,1,0:T(8,128)(2,1)S(1)}, u32[]{:S(2)}, u32[]{:S(2)}) collective-permute-start(bf16[3,48,128]{2,1,0:T(8,128)(2,1)S(1)} %get-tuple-element.621), channel_id=1, source_target_pairs={{0,1},{1,2},{2,3},{3,4},{4,5},{5,6},{6,7},{7,8},{8,9},{9,10},{10,1... | collective-permute-start | bytes 110600 | tf_op jit(solution)/shard_map/while/body/eval_jaxpr/ppermute | solution.py:63
  51.0 4.7 %collective-permute-start = (bf16[3,48,128]{2,1,0:T(8,128)(2,1)S(1)}, bf16[3,48,128]{2,1,0:T(8,128)(2,1)S(1)}, u32[]{:S(2)}, u32[]{:S(2)}) collective-permute-start(bf16[3,48,128]{2,1,0:T(8,128)(2,1)S(1)} %get-tuple-element.621), channel_id=1, source_target_pairs={{0,1},{1,2},{2,3},{3,4},{4,5},{5,6},{6,7},{7,8},{8,9},{9,10},{10,1... | collective-permute-start | bytes 110600 | tf_op jit(solution)/shard_map/while/body/eval_jaxpr/ppermute | solution.py:63
  58.7 4.7 %collective-permute-start = (bf16[3,48,128]{2,1,0:T(8,128)(2,1)S(1)}, bf16[3,48,128]{2,1,0:T(8,128)(2,1)S(1)}, u32[]{:S(2)}, u32[]{:S(2)}) collective-permute-start(bf16[3,48,128]{2,1,0:T(8,128)(2,1)S(1)} %get-tuple-element.621), channel_id=1, source_target_pairs={{0,1},{1,2},{2,3},{3,4},{4,5},{5,6},{6,7},{7,8},{8,9},{9,10},{10,1... | collective-permute-start | bytes 110600 | tf_op jit(solution)/shard_map/while/body/eval_jaxpr/ppermute | solution.py:63
  66.4 4.7 %collective-permute-start = (bf16[3,48,128]{2,1,0:T(8,128)(2,1)S(1)}, bf16[3,48,128]{2,1,0:T(8,128)(2,1)S(1)}, u32[]{:S(2)}, u32[]{:S(2)}) collective-permute-start(bf16[3,48,128]{2,1,0:T(8,128)(2,1)S(1)} %get-tuple-element.621), channel_id=1, source_target_pairs={{0,1},{1,2},{2,3},{3,4},{4,5},{5,6},{6,7},{7,8},{8,9},{9,10},{10,1... | collective-permute-start | bytes 110600 | tf_op jit(solution)/shard_map/while/body/eval_jaxpr/ppermute | solution.py:63
  71.5 7.3 %collective-permute-start = (bf16[3,48,128]{2,1,0:T(8,128)(2,1)S(1)}, bf16[3,48,128]{2,1,0:T(8,128)(2,1)S(1)}, u32[]{:S(2)}, u32[]{:S(2)}) collective-permute-start(bf16[3,48,128]{2,1,0:T(8,128)(2,1)S(1)} %get-tuple-element.621), channel_id=1, source_target_pairs={{0,1},{1,2},{2,3},{3,4},{4,5},{5,6},{6,7},{7,8},{8,9},{9,10},{10,1... | collective-permute-start | bytes 110600 | tf_op jit(solution)/shard_map/while/body/eval_jaxpr/ppermute | solution.py:63
  79.2 4.7 %collective-permute-start = (bf16[3,48,128]{2,1,0:T(8,128)(2,1)S(1)}, bf16[3,48,128]{2,1,0:T(8,128)(2,1)S(1)}, u32[]{:S(2)}, u32[]{:S(2)}) collective-permute-start(bf16[3,48,128]{2,1,0:T(8,128)(2,1)S(1)} %get-tuple-element.621), channel_id=1, source_target_pairs={{0,1},{1,2},{2,3},{3,4},{4,5},{5,6},{6,7},{7,8},{8,9},{9,10},{10,1... | collective-permute-start | bytes 110600 | tf_op jit(solution)/shard_map/while/body/eval_jaxpr/ppermute | solution.py:63
  84.2 4.7 %collective-permute-start = (bf16[3,48,128]{2,1,0:T(8,128)(2,1)S(1)}, bf16[3,48,128]{2,1,0:T(8,128)(2,1)S(1)}, u32[]{:S(2)}, u32[]{:S(2)}) collective-permute-start(bf16[3,48,128]{2,1,0:T(8,128)(2,1)S(1)} %get-tuple-element.621), channel_id=1, source_target_pairs={{0,1},{1,2},{2,3},{3,4},{4,5},{5,6},{6,7},{7,8},{8,9},{9,10},{10,1... | collective-permute-start | bytes 110600 | tf_op jit(solution)/shard_map/while/body/eval_jaxpr/ppermute | solution.py:63
  89.3 4.7 %collective-permute-start = (bf16[3,48,128]{2,1,0:T(8,128)(2,1)S(1)}, bf16[3,48,128]{2,1,0:T(8,128)(2,1)S(1)}, u32[]{:S(2)}, u32[]{:S(2)}) collective-permute-start(bf16[3,48,128]{2,1,0:T(8,128)(2,1)S(1)} %get-tuple-element.621), channel_id=1, source_target_pairs={{0,1},{1,2},{2,3},{3,4},{4,5},{5,6},{6,7},{7,8},{8,9},{9,10},{10,1... | collective-permute-start | bytes 110600 | tf_op jit(solution)/shard_map/while/body/eval_jaxpr/ppermute | solution.py:63
  94.4 4.7 %collective-permute-start = (bf16[3,48,128]{2,1,0:T(8,128)(2,1)S(1)}, bf16[3,48,128]{2,1,0:T(8,128)(2,1)S(1)}, u32[]{:S(2)}, u32[]{:S(2)}) collective-permute-start(bf16[3,48,128]{2,1,0:T(8,128)(2,1)S(1)} %get-tuple-element.621), channel_id=1, source_target_pairs={{0,1},{1,2},{2,3},{3,4},{4,5},{5,6},{6,7},{7,8},{8,9},{9,10},{10,1... | collective-permute-start | bytes 110600 | tf_op jit(solution)/shard_map/while/body/eval_jaxpr/ppermute | solution.py:63
  99.4 4.7 %collective-permute-start = (bf16[3,48,128]{2,1,0:T(8,128)(2,1)S(1)}, bf16[3,48,128]{2,1,0:T(8,128)(2,1)S(1)}, u32[]{:S(2)}, u32[]{:S(2)}) collective-permute-start(bf16[3,48,128]{2,1,0:T(8,128)(2,1)S(1)} %get-tuple-element.621), channel_id=1, source_target_pairs={{0,1},{1,2},{2,3},{3,4},{4,5},{5,6},{6,7},{7,8},{8,9},{9,10},{10,1... | collective-permute-start | bytes 110600 | tf_op jit(solution)/shard_map/while/body/eval_jaxpr/ppermute | solution.py:63
  104.5 4.7 %collective-permute-start = (bf16[3,48,128]{2,1,0:T(8,128)(2,1)S(1)}, bf16[3,48,128]{2,1,0:T(8,128)(2,1)S(1)}, u32[]{:S(2)}, u32[]{:S(2)}) collective-permute-start(bf16[3,48,128]{2,1,0:T(8,128)(2,1)S(1)} %get-tuple-element.621), channel_id=1, source_target_pairs={{0,1},{1,2},{2,3},{3,4},{4,5},{5,6},{6,7},{7,8},{8,9},{9,10},{10,1... | collective-permute-start | bytes 110600 | tf_op jit(solution)/shard_map/while/body/eval_jaxpr/ppermute | solution.py:63
  117.7 7.3 %collective-permute-start.4 = (f32[3,48,128]{2,1,0:T(8,128)}, f32[3,48,128]{2,1,0:T(8,128)S(1)}, u32[]{:S(2)}, u32[]{:S(2)}) collective-permute-start(f32[3,48,128]{2,1,0:T(8,128)} %get-tuple-element.654), channel_id=1, source_target_pairs={{0,1},{1,2},{2,3},{3,4},{4,5},{5,6},{6,7},{7,8},{8,9},{9,10},{10,1... | collective-permute-start | bytes 221192 | tf_op jit(solution)/shard_map/while/body/eval_jaxpr/ppermute | solution.py:89
  128.8 7.4 %collective-permute-start.4 = (f32[3,48,128]{2,1,0:T(8,128)}, f32[3,48,128]{2,1,0:T(8,128)S(1)}, u32[]{:S(2)}, u32[]{:S(2)}) collective-permute-start(f32[3,48,128]{2,1,0:T(8,128)} %get-tuple-element.654), channel_id=1, source_target_pairs={{0,1},{1,2},{2,3},{3,4},{4,5},{5,6},{6,7},{7,8},{8,9},{9,10},{10,1... | collective-permute-start | bytes 221192 | tf_op jit(solution)/shard_map/while/body/eval_jaxpr/ppermute | solution.py:89
  140.1 7.4 %collective-permute-start.4 = (f32[3,48,128]{2,1,0:T(8,128)}, f32[3,48,128]{2,1,0:T(8,128)S(1)}, u32[]{:S(2)}, u32[]{:S(2)}) collective-permute-start(f32[3,48,128]{2,1,0:T(8,128)} %get-tuple-element.654), channel_id=1, source_target_pairs={{0,1},{1,2},{2,3},{3,4},{4,5},{5,6},{6,7},{7,8},{8,9},{9,10},{10,1... | collective-permute-start | bytes 221192 | tf_op jit(solution)/shard_map/while/body/eval_jaxpr/ppermute | solution.py:89
  151.4 7.4 %collective-permute-start.4 = (f32[3,48,128]{2,1,0:T(8,128)}, f32[3,48,128]{2,1,0:T(8,128)S(1)}, u32[]{:S(2)}, u32[]{:S(2)}) collective-permute-start(f32[3,48,128]{2,1,0:T(8,128)} %get-tuple-element.654), channel_id=1, source_target_pairs={{0,1},{1,2},{2,3},{3,4},{4,5},{5,6},{6,7},{7,8},{8,9},{9,10},{10,1... | collective-permute-start | bytes 221192 | tf_op jit(solution)/shard_map/while/body/eval_jaxpr/ppermute | solution.py:89
  162.7 7.4 %collective-permute-start.4 = (f32[3,48,128]{2,1,0:T(8,128)}, f32[3,48,128]{2,1,0:T(8,128)S(1)}, u32[]{:S(2)}, u32[]{:S(2)}) collective-permute-start(f32[3,48,128]{2,1,0:T(8,128)} %get-tuple-element.654), channel_id=1, source_target_pairs={{0,1},{1,2},{2,3},{3,4},{4,5},{5,6},{6,7},{7,8},{8,9},{9,10},{10,1... | collective-permute-start | bytes 221192 | tf_op jit(solution)/shard_map/while/body/eval_jaxpr/ppermute | solution.py:89
  173.9 7.4 %collective-permute-start.4 = (f32[3,48,128]{2,1,0:T(8,128)}, f32[3,48,128]{2,1,0:T(8,128)S(1)}, u32[]{:S(2)}, u32[]{:S(2)}) collective-permute-start(f32[3,48,128]{2,1,0:T(8,128)} %get-tuple-element.654), channel_id=1, source_target_pairs={{0,1},{1,2},{2,3},{3,4},{4,5},{5,6},{6,7},{7,8},{8,9},{9,10},{10,1... | collective-permute-start | bytes 221192 | tf_op jit(solution)/shard_map/while/body/eval_jaxpr/ppermute | solution.py:89
  185.2 7.4 %collective-permute-start.4 = (f32[3,48,128]{2,1,0:T(8,128)}, f32[3,48,128]{2,1,0:T(8,128)S(1)}, u32[]{:S(2)}, u32[]{:S(2)}) collective-permute-start(f32[3,48,128]{2,1,0:T(8,128)} %get-tuple-element.654), channel_id=1, source_target_pairs={{0,1},{1,2},{2,3},{3,4},{4,5},{5,6},{6,7},{7,8},{8,9},{9,10},{10,1... | collective-permute-start | bytes 221192 | tf_op jit(solution)/shard_map/while/body/eval_jaxpr/ppermute | solution.py:89
  196.5 7.4 %collective-permute-start.4 = (f32[3,48,128]{2,1,0:T(8,128)}, f32[3,48,128]{2,1,0:T(8,128)S(1)}, u32[]{:S(2)}, u32[]{:S(2)}) collective-permute-start(f32[3,48,128]{2,1,0:T(8,128)} %get-tuple-element.654), channel_id=1, source_target_pairs={{0,1},{1,2},{2,3},{3,4},{4,5},{5,6},{6,7},{7,8},{8,9},{9,10},{10,1... | collective-permute-start | bytes 221192 | tf_op jit(solution)/shard_map/while/body/eval_jaxpr/ppermute | solution.py:89
  205.2 10.0 %collective-permute-start.4 = (f32[3,48,128]{2,1,0:T(8,128)}, f32[3,48,128]{2,1,0:T(8,128)S(1)}, u32[]{:S(2)}, u32[]{:S(2)}) collective-permute-start(f32[3,48,128]{2,1,0:T(8,128)} %get-tuple-element.654), channel_id=1, source_target_pairs={{0,1},{1,2},{2,3},{3,4},{4,5},{5,6},{6,7},{7,8},{8,9},{9,10},{10,1... | collective-permute-start | bytes 221192 | tf_op jit(solution)/shard_map/while/body/eval_jaxpr/ppermute | solution.py:89
  211.5 3.7 %collective-permute-start.5 = (f32[3,48,128]{2,1,0:T(8,128)}, f32[3,48,128]{2,1,0:T(8,128)S(1)}, u32[]{:S(2)}, u32[]{:S(2)}) collective-permute-start(f32[3,48,128]{2,1,0:T(8,128)} %get-tuple-element.655), channel_id=1, source_target_pairs={{0,1},{1,2},{2,3},{3,4},{4,5},{5,6},{6,7},{7,8},{8,9},{9,10},{10,1... | collective-permute-start | bytes 221192 | tf_op jit(solution)/shard_map/while/body/eval_jaxpr/ppermute | solution.py:89
  216.5 7.4 %collective-permute-start.4 = (f32[3,48,128]{2,1,0:T(8,128)}, f32[3,48,128]{2,1,0:T(8,128)S(1)}, u32[]{:S(2)}, u32[]{:S(2)}) collective-permute-start(f32[3,48,128]{2,1,0:T(8,128)} %get-tuple-element.654), channel_id=1, source_target_pairs={{0,1},{1,2},{2,3},{3,4},{4,5},{5,6},{6,7},{7,8},{8,9},{9,10},{10,1... | collective-permute-start | bytes 221192 | tf_op jit(solution)/shard_map/while/body/eval_jaxpr/ppermute | solution.py:89
  225.2 7.4 %collective-permute-start.4 = (f32[3,48,128]{2,1,0:T(8,128)}, f32[3,48,128]{2,1,0:T(8,128)S(1)}, u32[]{:S(2)}, u32[]{:S(2)}) collective-permute-start(f32[3,48,128]{2,1,0:T(8,128)} %get-tuple-element.654), channel_id=1, source_target_pairs={{0,1},{1,2},{2,3},{3,4},{4,5},{5,6},{6,7},{7,8},{8,9},{9,10},{10,1... | collective-permute-start | bytes 221192 | tf_op jit(solution)/shard_map/while/body/eval_jaxpr/ppermute | solution.py:89
  233.8 7.4 %collective-permute-start.4 = (f32[3,48,128]{2,1,0:T(8,128)}, f32[3,48,128]{2,1,0:T(8,128)S(1)}, u32[]{:S(2)}, u32[]{:S(2)}) collective-permute-start(f32[3,48,128]{2,1,0:T(8,128)} %get-tuple-element.654), channel_id=1, source_target_pairs={{0,1},{1,2},{2,3},{3,4},{4,5},{5,6},{6,7},{7,8},{8,9},{9,10},{10,1... | collective-permute-start | bytes 221192 | tf_op jit(solution)/shard_map/while/body/eval_jaxpr/ppermute | solution.py:89
  242.5 7.4 %collective-permute-start.4 = (f32[3,48,128]{2,1,0:T(8,128)}, f32[3,48,128]{2,1,0:T(8,128)S(1)}, u32[]{:S(2)}, u32[]{:S(2)}) collective-permute-start(f32[3,48,128]{2,1,0:T(8,128)} %get-tuple-element.654), channel_id=1, source_target_pairs={{0,1},{1,2},{2,3},{3,4},{4,5},{5,6},{6,7},{7,8},{8,9},{9,10},{10,1... | collective-permute-start | bytes 221192 | tf_op jit(solution)/shard_map/while/body/eval_jaxpr/ppermute | solution.py:89
  251.2 7.4 %collective-permute-start.4 = (f32[3,48,128]{2,1,0:T(8,128)}, f32[3,48,128]{2,1,0:T(8,128)S(1)}, u32[]{:S(2)}, u32[]{:S(2)}) collective-permute-start(f32[3,48,128]{2,1,0:T(8,128)} %get-tuple-element.654), channel_id=1, source_target_pairs={{0,1},{1,2},{2,3},{3,4},{4,5},{5,6},{6,7},{7,8},{8,9},{9,10},{10,1... | collective-permute-start | bytes 221192 | tf_op jit(solution)/shard_map/while/body/eval_jaxpr/ppermute | solution.py:89
  259.9 7.4 %collective-permute-start.4 = (f32[3,48,128]{2,1,0:T(8,128)}, f32[3,48,128]{2,1,0:T(8,128)S(1)}, u32[]{:S(2)}, u32[]{:S(2)}) collective-permute-start(f32[3,48,128]{2,1,0:T(8,128)} %get-tuple-element.654), channel_id=1, source_target_pairs={{0,1},{1,2},{2,3},{3,4},{4,5},{5,6},{6,7},{7,8},{8,9},{9,10},{10,1... | collective-permute-start | bytes 221192 | tf_op jit(solution)/shard_map/while/body/eval_jaxpr/ppermute | solution.py:89
  268.6 6.8 %collective-permute-start.6 = (f32[3,48,128]{2,1,0:T(8,128)}, f32[3,48,128]{2,1,0:T(8,128)S(1)}, u32[]{:S(2)}, u32[]{:S(2)}) collective-permute-start(f32[3,48,128]{2,1,0:T(8,128)} %get-tuple-element.410), channel_id=1, source_target_pairs={{0,1},{1,2},{2,3},{3,4},{4,5},{5,6},{6,7},{7,8},{8,9},{9,10},{10,1... | collective-permute-start | bytes 221192 | tf_op jit(solution)/shard_map/ppermute | solution.py:94
  (68 other events, 267.5 us)
where the time goes:
time: 278 us; the launch traced here: 277 us
  starting transfers between devices  121 us (44%)
  waiting for transfers between devices  55.8 us (20%)
  matrix products  42.6 us (15%)
  local copies, waits for them, and re-layouts  41.4 us (15%)
  other arithmetic  13.8 us (5%)
    ppermute x60, starting transfers between devices, backward_step(): lax.ppermute((key_blk, value_blk, dkey_blk, dvalue_blk), 'cp', shift_pairs)  59.5 us
    ppermute x30, starting transfers between devices, forward_step(): key_blk, value_blk = lax.ppermute((key_blk, value_blk), 'cp', shift_pairs)  58.1 us
    while x90, local copies, waits for them, and re-layouts  37.5 us
    ppermute x60, waiting for transfers between devices, backward_step(): lax.ppermute((key_blk, value_blk, dkey_blk, dvalue_blk), 'cp', shift_pairs)  35.8 us
    ppermute x30, waiting for transfers between devices, forward_step(): key_blk, value_blk = lax.ppermute((key_blk, value_blk), 'cp', shift_pairs)  20 us
    dot_general x15, matrix products, block_scores(): jnp.einsum('crie,cle->cril', query_rot, key_blk, preferred_element_type=j...  14.6 us
    dot_general x8, matrix products, forward_block(): jnp.einsum('cril,cle->crie', weights.astype(jnp.bfloat16), value_blk, pre...  8.81 us
    dot_general x8, matrix products, backward_block(): jnp.einsum('crie,cle->cril', grad_out, value_blk, preferred_element_type=...  5.57 us
  transfers between devices with their start and end apart: 92, of which 45 were waited for; matrix products, arithmetic and copies ran while one was open for 8% of the time, Pallas kernels for 0%

commit v1 on v0

v1 whole, which is shorter than its diff:
```python
import functools

import jax
import jax.numpy as jnp
from jax import lax
from jax.experimental import pallas as pl
from jax.experimental.pallas import tpu as pltpu
from jax.sharding import PartitionSpec as P

ROPE_BASE = 10000
LOG2E = 1.4426950408889634
TILE_TOKENS = 8


def rope_tables(positions, head):
    half_dim = head // 2
    inv_freq = jnp.power(jnp.float32(ROPE_BASE), -2.0 * jnp.arange(half_dim, dtype=jnp.float32) / head)
    angles = positions.astype(jnp.float32)[..., None] * inv_freq
    angles = jnp.concatenate([angles, angles], axis=-1)
    return jnp.cos(angles), jnp.sin(angles)


def compute_kernel(pad_heads, scale, q_ref, do_ref, kv_ref, cos_ref, sin_ref, out_ref, dq_ref, part_ref, qn, don, padf, p_buf, ds_buf):
    batch, blk, heads, head = q_ref.shape
    keys = kv_ref.shape[2]
    rows = blk * pad_heads
    tile = TILE_TOKENS * pad_heads
    me = lax.axis_index('cp')
    padf[:, heads:, :] = jnp.zeros((blk, pad_heads - heads, head), jnp.float32)
    cos = cos_ref[...][:, None, :]
    sin = sin_ref[...][:, None, :]

    def prep(b, carry):
        padf[:, :heads, :] = q_ref[b].astype(jnp.float32)
        x = padf[...]
        turned = pltpu.roll(x.reshape(rows, head), head // 2, 1).reshape(blk, pad_heads, head)
        qn[b] = (x * cos + turned * sin).reshape(rows, head).astype(jnp.bfloat16)
        padf[:, :heads, :] = do_ref[b].astype(jnp.float32)
        don[b] = padf[...].reshape(rows, head).astype(jnp.bfloat16)
        return carry

    lax.fori_loop(0, batch, prep, 0)

    def attend(step, carry):
        b = step // (blk // TILE_TOKENS)
        i = step % (blk // TILE_TOKENS)
        row0 = pl.multiple_of(i * tile, tile)
        q_t = qn[b, pl.ds(row0, tile), :]
        do_t = don[b, pl.ds(row0, tile), :]
        k_all = kv_ref[b, 0]
        v_all = kv_ref[b, 1]
        nt = (((1,), (1,)), ((), ()))
        s = lax.dot_general(q_t, k_all, nt, preferred_element_type=jnp.float32)
        tok = lax.broadcasted_iota(jnp.int32, (TILE_TOKENS, pad_heads, 1), 0).reshape(tile, 1) + (me * blk + i * TILE_TOKENS)
        col = lax.broadcasted_iota(jnp.int32, (tile, keys), 1)
        s = jnp.where(col <= tok, s, -jnp.inf)
        m = jnp.max(s, axis=1, keepdims=True)
        e = jnp.exp2((s - m) * (scale * LOG2E))
        inv_l = 1.0 / jnp.sum(e, axis=1, keepdims=True)
        o = jnp.dot(e.astype(jnp.bfloat16), v_all, preferred_element_type=jnp.float32) * inv_l
        ob = o.astype(jnp.bfloat16)
        of = ob.astype(jnp.float32)
        out_ref[b, pl.ds(i * TILE_TOKENS, TILE_TOKENS)] = of.reshape(TILE_TOKENS, pad_heads, head)[:, :heads, :].astype(jnp.bfloat16)
        delta = jnp.sum(do_t.astype(jnp.float32) * of, axis=1, keepdims=True)
        dp = lax.dot_general(do_t, v_all, nt, preferred_element_type=jnp.float32)
        p = e * inv_l
        p_buf[b, pl.ds(row0, tile), :] = p.astype(jnp.bfloat16)
        ds_buf[b, pl.ds(row0, tile), :] = (p * (dp - delta)).astype(jnp.bfloat16)
        return carry

    def key_grads(b):
        tn = (((0,), (0,)), ((), ()))
        dkt = lax.dot_general(qn[b], ds_buf[b], tn, preferred_element_type=jnp.float32)
        part_ref[b, 0] = dkt.T * scale
        dvt = lax.dot_general(don[b], p_buf[b], tn, preferred_element_type=jnp.float32)
        part_ref[b, 1] = dvt.T

    def query_grads(step, carry):
        b = step // (blk // TILE_TOKENS)
        i = step % (blk // TILE_TOKENS)
        row0 = pl.multiple_of(i * tile, tile)
        g = jnp.dot(ds_buf[b, pl.ds(row0, tile), :], kv_ref[b, 0], preferred_element_type=jnp.float32) * scale
        turned = pltpu.roll(g, head // 2, 1).reshape(TILE_TOKENS, pad_heads, head)
        cos_t = cos_ref[pl.ds(i * TILE_TOKENS, TILE_TOKENS), :][:, None, :]
        sin_t = sin_ref[pl.ds(i * TILE_TOKENS, TILE_TOKENS), :][:, None, :]
        g = g.reshape(TILE_TOKENS, pad_heads, head) * cos_t - turned * sin_t
        dq_ref[b, pl.ds(i * TILE_TOKENS, TILE_TOKENS)] = g[:, :heads, :].astype(jnp.bfloat16)
        return carry

    tiles = blk // TILE_TOKENS

    def one_batch(b, carry):
        lax.fori_loop(b * tiles, (b + 1) * tiles, attend, 0)
        key_grads(b)
        lax.fori_loop(b * tiles, (b + 1) * tiles, query_grads, 0)
        return carry

    lax.fori_loop(0, batch, one_batch, 0)


def solution(mesh):
    query_spec = P('dp', 'cp', None, None)
    kv_spec = P('dp', 'cp', None)
    pos_spec = P(('dp', 'cp'))
    cp_size = mesh.shape['cp']

    def per_device(query, key, value, positions, grad_out):
        batch, blk, heads, head = query.shape
        scale = head ** -0.5
        pad_heads = -(-heads // 8) * 8
        rows = blk * pad_heads
        keys = cp_size * blk
        cos_tab, sin_tab = rope_tables(positions, head)
        sin_signed = jnp.where(jnp.arange(head) < head // 2, -sin_tab, sin_tab)
        kf = key.astype(jnp.float32)
        turned = jnp.roll(kf, head // 2, axis=-1)
        key_rot = (kf * cos_tab[None] + turned * sin_signed[None]).astype(jnp.bfloat16)
        kv = lax.all_gather(jnp.stack([key_rot, value], axis=1), 'cp', axis=2, tiled=True)
        vm = pl.BlockSpec(memory_space=pltpu.VMEM)
        attn, dq, part = pl.pallas_call(
            functools.partial(compute_kernel, pad_heads, scale),
            out_shape=(
                jax.ShapeDtypeStruct(query.shape, jnp.bfloat16),
                jax.ShapeDtypeStruct(query.shape, jnp.bfloat16),
                jax.ShapeDtypeStruct((batch, 2, keys, head), jnp.float32),
            ),
            in_specs=[vm] * 5,
            out_specs=(vm, vm, vm),
            scratch_shapes=[
                pltpu.VMEM((batch, rows, head), jnp.bfloat16),
                pltpu.VMEM((batch, rows, head), jnp.bfloat16),
                pltpu.VMEM((blk, pad_heads, head), jnp.float32),
                pltpu.VMEM((batch, rows, keys), jnp.bfloat16),
                pltpu.VMEM((batch, rows, keys), jnp.bfloat16),
            ],
            compiler_params=pltpu.CompilerParams(vmem_limit_bytes=60 * 2**20),
        )(query, grad_out, kv, cos_tab, sin_signed)
        home = lax.psum_scatter(part, 'cp', scatter_dimension=2, tiled=True)
        gk = home[:, 0]
        gk = gk * cos_tab[None] - jnp.roll(gk, head // 2, axis=-1) * sin_signed[None]
        return attn, dq, gk.astype(jnp.bfloat16), home[:, 1].astype(jnp.bfloat16)

    return jax.shard_map(per_device, mesh=mesh, in_specs=(query_spec, kv_spec, kv_spec, pos_spec, query_spec), out_specs=(query_spec, query_spec, kv_spec, kv_spec), check_vma=False)
```

time: 278 us -> 146 us (0.53)
  starting transfers between devices: 121 us -> 0.13 us
  matrix products: 42.6 us -> 0 us
  waiting for transfers between devices: 55.8 us -> 86.9 us
  local copies, waits for them, and re-layouts: 41.4 us -> 13.2 us
  Pallas kernels: 0 us -> 24.2 us
  between operations: 0.79 us -> 14.1 us
  other arithmetic: 13.8 us -> 4.85 us
    ppermute x92 -> x0, starting transfers between devices: 121 us -> none  [the longest x60 59.5 us: backward_step(): lax.ppermute((key_blk, value_blk, dkey_blk, dvalue_blk), 'cp', shift_pairs)]
    ppermute x92 -> x0, waiting for transfers between devices: 55.8 us -> none  [the longest x60 35.8 us: backward_step(): lax.ppermute((key_blk, value_blk, dkey_blk, dvalue_blk), 'cp', shift_pairs)]
    reduce_scatter x0 -> x1, waiting for transfers between devices: none -> 53 us  [per_device(): home = lax.psum_scatter(part, 'cp', scatter_dimension=2, tiled=True)]
    dot_general x55 -> x0, matrix products: 42.6 us -> none  [the longest x15 14.6 us: block_scores(): jnp.einsum('crie,cle->cril', query_rot, key_blk, preferred_element_type=j...]
    while x90 -> x0, local copies, waits for them, and re-layouts: 37.5 us -> none
    all_gather x0 -> x1, waiting for transfers between devices: none -> 33.8 us  [per_device(): lax.all_gather(jnp.stack([key_rot, value], axis=1), 'cp', axis=2, tiled=T...]
    pallas_call x0 -> x1, Pallas kernels: none -> 24.2 us  [per_device(): pl.pallas_call(functools.partial(compute_kernel, pad_heads, scale), out_s...]
    reduce_sum x8 -> x0, other arithmetic: 3.51 us -> none  [forward_block(): run_sum = run_sum * factor + jnp.sum(weights, axis=-1)]
  transfers between devices with their start and end apart: 92 -> 2, of which waited for: 45 -> 2; matrix products, arithmetic and copies ran while one was open for 8% -> 4% of each run, Pallas kernels for 0% -> 0%
where the time goes in v1:
time: 146 us; the launch traced here: 143 us
  waiting for transfers between devices  86.9 us (60%)
  Pallas kernels  24.2 us (17%)
  between operations  14.1 us (10%)
  local copies, waits for them, and re-layouts  13.2 us (9%)
  other arithmetic  4.85 us (3%)
    reduce_scatter x1, waiting for transfers between devices, per_device(): home = lax.psum_scatter(part, 'cp', scatter_dimension=2, tiled=True)  53 us
    all_gather x1, waiting for transfers between devices, per_device(): lax.all_gather(jnp.stack([key_rot, value], axis=1), 'cp', axis=2, tiled=T...  33.8 us
    pallas_call x1, Pallas kernels, per_device(): pl.pallas_call(functools.partial(compute_kernel, pad_heads, scale), out_s...  24.2 us
    unnamed x18, local copies, waits for them, and re-layouts  6.58 us
    pallas_call x1, local copies, waits for them, and re-layouts, per_device(): pl.pallas_call(functools.partial(compute_kernel, pad_heads, scale), out_s...  3.25 us
  transfers between devices with their start and end apart: 2, of which 2 were waited for; matrix products, arithmetic and copies ran while one was open for 4% of the time, Pallas kernels for 0%

profile of v1, /device:TPU:119, one launch (start us, length us, event | category | flops | bytes accessed | tf_op | source)
XLA Modules:
  0.0 143.5 jit_solution(2688434711666767465)
XLA Ops:
  7.2 0.0 copy-start.2
  7.2 0.1 all-gather.2.cloned.1.call-start
  7.3 0.7 convert_element_type.17
  8.0 0.9 fusion.8
  8.9 0.1 broadcast_multiply_fusion
  9.0 0.2 fusion.6
  9.2 0.0 copy-start.3
  9.2 0.0 copy-start.5
  9.2 0.9 fusion.4
  10.1 1.4 pad_maximum_fusion
  11.5 0.1 all-gather.2.cloned.1.call-update
  11.5 0.1 reduce-scatter.2.cloned.1.call-start
  11.6 2.3 %copy.9.q_ref = bf16[3,48,22,128]{3,2,1,0:T(8,128)(2,1)} copy(bf16[3,48,22,128]{3,1,2,0:T(8,128)(2,1)} %param.5) | data formatting | bytes 1622016 | tf_op args[0]
  13.9 0.0 copy-done.2
  13.9 1.2 copy.10.do_ref
  15.1 33.8 %all-gather.2.cloned.1.call-done.kv_ref = bf16[3,2,768,128]{3,2,1,0:T(8,128)(2,1)} async-done(((bf16[3,2,48,128]{3,2,1,0:T(8,128)(2,1)}), bf16[3,2,768,128]{3,2,1,0:T(8,128)(2,1)}) %all-gather.2.cloned.1.call-update) | async-done | bytes 1179664 | tf_op jit(solution)/shard_map/all_gather | solution.py:118
  48.9 0.0 copy-done.3
  48.9 0.0 copy-done.5
  48.9 24.2 %shard_map.84 = (bf16[3,48,22,128]{3,2,1,0:T(8,128)(2,1)}, bf16[3,48,22,128]{3,2,1,0:T(8,128)(2,1)}, f32[3,2,768,128]{3,2,1,0:T(8,128)}) custom-call(bf16[3,48,22,128]{3,2,1,0:T(8,128)(2,1)} %copy.9.q_ref, bf16[3,48,22,128]{3,2,1,0:T(8,128)(2,1)} %copy.10.do_ref, bf16[3,2,768,128]{3,2,1,0:T(8,128)(2,1)} %all-gather.2.cloned.1.call-done.kv_ref, ...), custom_call_target="tpu_custom_call" | custom-call | tf_op jit(solution)/shard_map/pallas_call | solution.py:120
  73.1 3.2 %copy.11 = f32[3,2,768,128]{3,2,0,1:T(8,128)} copy(f32[3,2,768,128]{3,2,1,0:T(8,128)} %get-tuple-element.9) | data formatting | bytes 4718592 | tf_op jit(solution)/shard_map/pallas_call | solution.py:120
  76.3 0.1 reduce-scatter.2.cloned.1.call-update
  76.4 0.0 copy-start.4
  76.4 0.0 copy-start.6
  76.4 1.1 copy-done.1
  77.5 1.0 copy.12
  78.5 1.0 copy.13
  79.5 53.0 %reduce-scatter.2.cloned.1.call-done = f32[3,2,48,128]{3,2,0,1:T(8,128)} async-done(((f32[3,2,768,128]{3,2,0,1:T(8,128)}), f32[3,2,48,128]{3,2,0,1:T(8,128)}) %reduce-scatter.2.cloned.1.call-update) | async-done | bytes 147472 | tf_op jit(solution)/shard_map/reduce_scatter | solution.py:138
  132.5 0.9 slice_bitcast_fusion
  133.4 0.1 fusion.7
  133.5 1.5 %fusion.5 = bf16[3,48,128]{2,1,0:T(8,128)(2,1)} fusion(f32[3,2,48,128]{3,2,0,1:T(8,128)} %reduce-scatter.2.cloned.1.call-done), kind=kLoop, calls=%fused_computation.11 | loop fusion | bytes 73728 | tf_op jit(solution)/shard_map/convert_element_type | solution.py:141
  135.0 0.0 copy-done.4
  135.0 1.6 %fusion.3 = bf16[3,48,128]{2,1,0:T(8,128)(2,1)} fusion(f32[3,48,64]{2,1,0:T(8,128)S(1)} %get-tuple-element.15, f32[3,48,64]{2,1,0:T(8,128)S(1)} %get-tuple-element.14, f32[48,128]{1,0:T(8,128)S(1)} %copy-done.6, f32[48,128]{1,0:T(8,128)S(1)} %copy-done.4, f32[3,2,48,128]{3,2,0,1:T(8,128)} %reduce-scatter.2.cloned.1.call-done), kind=kLoop, calls=%fused_computation.8 | loop fusion | flops 92160 | bytes 233472 | tf_op jit(solution)/shard_map/convert_element_type | solution.py:141
  (6 shorter events, 0.0 us)
Async XLA Ops:
  7.2 6.8 %copy-start.2 = (bf16[3,48,22,128]{3,1,2,0:T(8,128)(2,1)S(1)}, bf16[3,48,22,128]{3,1,2,0:T(8,128)(2,1)}, u32[]{:S(2)}) copy-start(bf16[3,48,22,128]{3,1,2,0:T(8,128)(2,1)} %param.9) | copy-start | bytes 2433028
  7.2 41.7 %all-gather.2.cloned.1.call-start = ((), (), s32[]{:S(2)}) async-start(), calls=%async_computation.1 | async-start | bytes 1253376 | tf_op jit(solution)/shard_map/all_gather | solution.py:118
  9.2 39.7 %copy-start.3 = (f32[48,128]{1,0:T(8,128)}, f32[48,128]{1,0:T(8,128)S(1)}, u32[]{:S(2)}) copy-start(f32[48,128]{1,0:T(8,128)S(1)} %get-tuple-element.18.cos_ref) | copy-start | bytes 73732
  9.2 39.7 %copy-start.5 = (f32[48,128]{1,0:T(8,128)}, f32[48,128]{1,0:T(8,128)S(1)}, u32[]{:S(2)}) copy-start(f32[48,128]{1,0:T(8,128)S(1)} %get-tuple-element.19.sin_ref) | copy-start | bytes 73732
  11.5 121.0 %reduce-scatter.2.cloned.1.call-start = ((), (), s32[]{:S(2)}) async-start(), calls=%async_computation.2 | async-start | bytes 2506752 | tf_op jit(solution)/shard_map/reduce_scatter | solution.py:138
  76.3 1.2 copy-start.1
  76.3 2.2 %copy-start = (bf16[3,48,22,128]{3,2,1,0:T(8,128)(2,1)S(1)}, bf16[3,48,22,128]{3,2,1,0:T(8,128)(2,1)}, u32[]{:S(2)}) copy-start(bf16[3,48,22,128]{3,2,1,0:T(8,128)(2,1)} %get-tuple-element.11) | copy-start | bytes 2433028
  76.4 58.6 %copy-start.4 = (f32[48,128]{1,0:T(8,128)S(1)}, f32[48,128]{1,0:T(8,128)}, u32[]{:S(2)}) copy-start(f32[48,128]{1,0:T(8,128)} %copy-done.3) | copy-start | bytes 73732
  76.4 58.6 %copy-start.6 = (f32[48,128]{1,0:T(8,128)S(1)}, f32[48,128]{1,0:T(8,128)}, u32[]{:S(2)}) copy-start(f32[48,128]{1,0:T(8,128)} %copy-done.5) | copy-start | bytes 73732
Sparse Core Ops, SparseCore 0:
  11.7 37.1 all-gather.1
  76.5 55.9 reduce-scatter.1
